TPU v7x, 32 devices: a whole 2x2x4 slice. The times are simulated.
32 devices in a mesh: dp: 8 (over z, x), tp: 4 (over y, core).
Axes of the slice: x: 2, y: 2, z: 4, core: 2. Of those that a mesh axis runs over, the one named last changes fastest.
Arguments:
- queries: bfloat16 [4096, 8192], P('dp', 'tp'), parts along dimension 0, may hold values from -200 to 200
- new_keys: bfloat16 [4096, 1024], P('dp', 'tp'), parts along dimension 0, may hold values from -9 to 9
- new_values: bfloat16 [4096, 1024], P('dp', 'tp'), parts along dimension 0, may hold values from -60 to 60
- cache_keys: bfloat16 [32, 32768, 128], P('dp', 'tp'), parts along dimension 0, may hold values from -4 to 4
- cache_values: bfloat16 [32, 32768, 128], P('dp', 'tp'), parts along dimension 0, may hold values from -60 to 60
- out_weight: bfloat16 [8192, 8192], P('tp'), may hold values from -0.09375 to 0.09375
- residual: bfloat16 [4096, 8192], P('dp', 'tp'), parts along dimension 0, may hold values from -8 to 8
- norm_gain: bfloat16 [8192], P('tp'), may hold values from 0.5 to 1.5
Outputs:
- normed: bfloat16 [4096, 8192], P('dp', 'tp'), parts along dimension 0
There are 8 independent parts, one for each index of `dp`. A program takes and returns all parts, laid end to end along the dimension named above; an argument that names none is the same for every part. Nothing has to cross between parts.
All inputs are finite; a program needn't handle non-finite values.
Results may differ from a plain program's by a relative error of at most 0.015.
Values may be sent and summed in bfloat16 or wider, within the bound.
A program may use at most 256 MiB of HBM per device.

v0:
```python
import jax
import jax.numpy as jnp
from jax import lax
from jax.sharding import PartitionSpec as P

D = 8192
KVH = 8
HD = 128
SPAN = 128
SEQS = 4
CTX = 4096


EPSILON = 1e-05


def partner(value, axis, bit):
    mask = 2**bit
    pairs = [(source, source ^ mask) for source in range(lax.axis_size(axis))]
    return lax.ppermute(value, axis, pairs)


def attend_block(query_rows, stored_keys, stored_values, fresh_keys, fresh_values, local_kv):
    heads_here = query_rows.shape[1] // HD
    groups = heads_here // local_kv
    length = stored_keys.shape[1] // local_kv
    scaling = HD ** (-0.5)
    grouped = query_rows.reshape(SEQS, SPAN, local_kv, groups, HD)
    old_keys = stored_keys.reshape(SEQS, local_kv, length, HD)
    old_values = stored_values.reshape(SEQS, local_kv, length, HD)
    scores = (
        jnp.einsum("sighd,sgjd->sghij", grouped, old_keys, preferred_element_type=jnp.float32)
        * scaling
    )
    peak = jnp.max(scores, axis=-1)
    recent_keys = fresh_keys.reshape(SEQS, SPAN, local_kv, HD)
    recent_values = fresh_values.reshape(SEQS, SPAN, local_kv, HD)
    recent_scores = (
        jnp.einsum("sighd,sjgd->sghij", grouped, recent_keys, preferred_element_type=jnp.float32)
        * scaling
    )
    causal = jnp.arange(SPAN)[:, None] >= jnp.arange(SPAN)[None, :]
    recent_scores = jnp.where(causal, recent_scores, -jnp.inf)
    peak = jnp.maximum(peak, jnp.max(recent_scores, axis=-1))
    weights = jnp.exp(scores - peak[..., None])
    total = jnp.sum(weights, axis=-1)
    mixed = jnp.einsum(
        "sghij,sgjd->sighd",
        weights.astype(jnp.bfloat16),
        old_values,
        preferred_element_type=jnp.float32,
    )
    recent_weights = jnp.exp(recent_scores - peak[..., None])
    total = total + jnp.sum(recent_weights, axis=-1)
    mixed = mixed + jnp.einsum(
        "sghij,sjgd->sighd",
        recent_weights.astype(jnp.bfloat16),
        recent_values,
        preferred_element_type=jnp.float32,
    )
    return (mixed, peak, total)


def token_layout(stat):
    return jnp.transpose(stat, (0, 3, 1, 2))[..., None]


def finish_rows(mixed, total):
    result = mixed / token_layout(total)
    return result.reshape(SEQS * SPAN, -1).astype(jnp.bfloat16)


def per_device(
    queries, new_keys, new_values, cache_keys, cache_values, out_weight, residual, norm_gain
):
    tp_size = lax.axis_size("tp")
    paired = tp_size == 2 * KVH
    local_kv = 1 if paired else cache_keys.shape[1] // CTX
    parity = lax.axis_index("tp") % 2

    def join_dims(own_piece, other_piece):
        first = jnp.concatenate([own_piece, other_piece], axis=-1)
        second = jnp.concatenate([other_piece, own_piece], axis=-1)
        return jnp.where(parity == 0, first, second)

    if paired:
        other_keys, other_values, other_stored_keys, other_stored_values = partner(
            (new_keys, new_values, cache_keys, cache_values), "tp", 0
        )
        fresh_keys = join_dims(new_keys, other_keys)
        fresh_values = join_dims(new_values, other_values)
        stored_keys = jnp.concatenate([cache_keys, other_stored_keys], axis=1)
        stored_values = jnp.concatenate([cache_values, other_stored_values], axis=1)
    else:
        fresh_keys, fresh_values = (new_keys, new_values)
        stored_keys, stored_values = (cache_keys, cache_values)
    mixed, peak, total = attend_block(
        queries, stored_keys, stored_values, fresh_keys, fresh_values, local_kv
    )
    attended = finish_rows(mixed, total)
    projected = lax.psum_scatter(
        lax.dot_general(
            out_weight, attended, (((0,), (1,)), ((), ())), preferred_element_type=jnp.float32
        ).astype(jnp.bfloat16),
        "tp",
        scatter_dimension=0,
        tiled=True,
    ).astype(jnp.float32)
    hidden = residual.astype(jnp.float32) + jnp.transpose(projected)
    squares = lax.psum(jnp.sum(hidden * hidden, axis=1), "tp")
    scaled = (
        hidden * lax.rsqrt(squares / D + EPSILON)[:, None] * norm_gain.astype(jnp.float32)[None, :]
    )
    return scaled.astype(jnp.bfloat16)


def solution(mesh):
    in_specs = (
        P("dp", "tp"),
        P("dp", "tp"),
        P("dp", "tp"),
        P("dp", "tp", None),
        P("dp", "tp", None),
        P("tp", None),
        P("dp", "tp"),
        P("tp"),
    )
    out_specs = P("dp", "tp")
    return jax.shard_map(
        per_device, mesh=mesh, in_specs=in_specs, out_specs=out_specs, check_vma=False
    )
```

profile of v0, /device:TPU:0, one launch (start us, length us, event | category | flops | bytes accessed | tf_op | source)
XLA Modules:
  0.0 276.8 jit_solution(12630912312721364948)
XLA Ops:
  6.5 0.0 copy-start.2
  6.5 0.0 reduce-scatter.2.cloned.1.call-start
  6.6 2.2 copy.32
  8.8 0.0 copy-done.2
  8.8 0.1 reshape.27
  8.9 47.0 %bitcast_reduce_fusion = (f32[4,2,8,128]{3,2,1,0:T(8,128)S(1)}, f32[4,2,4096,128,8]{3,2,4,1,0:T(8,128)}) fusion(bf16[4,2,4096,128,1]{3,2,4,1,0:T(8,128)(2,1)} %bitcast.56, bf16[4,128,2,8,128]{4,3,2,1,0:T(8,128)(2,1)S(1)} %bitcast.54), kind=kOutput, calls=%fused_computation.1 | convolution fusion | flops 8657035264 | bytes 144736256 | tf_op jit(solution)/shard_map/sighd,sgjd->sghij/dot_general | solution.py:32
  55.9 1.0 fusion.9
  56.9 0.0 copy-start
  56.9 1.9 copy-done
  58.9 1.2 fusion.7
  60.0 40.9 %fusion.1 = f32[4,2,8,128]{3,2,1,0:T(8,128)S(1)} fusion(f32[4,2,4096,128,8]{3,2,4,1,0:T(8,128)} %get-tuple-element.6, f32[4,2,8,128]{3,2,1,0:T(8,128)S(1)} %max.7), kind=kLoop, calls=%fused_computation.3 | loop fusion | flops 100655104 | bytes 134283264 | tf_op jit(solution)/shard_map/reduce_sum | solution.py:46
  101.0 0.0 copy-start.3
  101.0 48.1 %fusion.3 = f32[4,2,8,128,128]{4,3,2,1,0:T(8,128)} fusion(bf16[4,2,4096,128,1]{3,2,4,1,0:T(8,128)(2,1)} %bitcast.57, f32[4,2,4096,128,8]{3,2,4,1,0:T(8,128)} %get-tuple-element.6, f32[4,2,8,128]{3,2,1,0:T(8,128)S(1)} %max.7), kind=kOutput, calls=%fused_computation.5 | convolution fusion | flops 8690597888 | bytes 146833408 | tf_op jit(solution)/shard_map/sghij,sgjd->sighd/dot_general | solution.py:47
  149.1 0.0 copy-done.3
  149.1 0.1 reshape.29
  149.2 4.8 %fusion.6 = bf16[4,128,2,8,128]{4,1,3,2,0:T(8,128)(2,1)S(1)} fusion(f32[4,2,8,128,128]{4,3,2,1,0:T(8,128)} %fusion.3, f32[4,2,128,128,8]{3,2,4,1,0:T(8,128)} %copy-done, f32[4,128,2,8]{1,3,2,0:T(8,128)S(1)} %add_bitcast_fusion, f32[4,2,8,128]{3,2,1,0:T(8,128)S(1)} %max.7, pred[128,128]{0,1:T(8,128)(4,1)S(1)} %iota_compare_fusion, ...), kind=kOutput, calls=%fused_computation.10 | convolution fusion | flops 275775488 | bytes 10829824 | tf_op jit(solution)/shard_map/sghij,sjgd->sighd/dot_general | solution.py:55
  154.0 1.4 copy.21
  155.4 2.3 convert_element_type.32
  157.7 26.1 %fusion.5 = bf16[8192,512]{0,1:T(8,128)(2,1)} fusion(bf16[512,2048]{1,0:T(8,128)(2,1)} %convert_element_type.32, bf16[2048,8192]{1,0:T(8,128)(2,1)} %param.13), kind=kOutput, calls=%fused_computation.7 | convolution fusion | flops 17184063488 | bytes 44040192 | tf_op jit(solution)/shard_map/dot_general | solution.py:102
  183.7 0.0 copy-start.4
  183.7 0.0 copy-start.1
  183.7 0.0 reduce-scatter.2.cloned.1.call-update
  183.8 0.7 copy-done.4
  184.4 73.5 %reduce-scatter.2.cloned.1.call-done = bf16[2048,512]{0,1:T(8,128)(2,1)} async-done(((bf16[8192,512]{0,1:T(8,128)(2,1)}), bf16[2048,512]{0,1:T(8,128)(2,1)}) %reduce-scatter.2.cloned.1.call-update) | async-done | bytes 2097168 | tf_op jit(solution)/shard_map/reduce_scatter | solution.py:101
  257.9 0.0 copy-done.1
  257.9 2.3 multiply_reduce_fusion
  260.2 5.8 %psum.7 = f32[512]{0:T(512)S(1)} all-reduce(f32[512]{0:T(512)S(1)} %multiply_reduce_fusion), channel_id=1, replica_groups=mesh['dp'=8,'tp'=4] {'tp'}, use_global_device_ids=true, to_apply=%region_6.7 | all-reduce | flops 512 | bytes 4096 | tf_op jit(solution)/shard_map/psum | solution.py:110
  266.0 4.0 %multiply_convert_fusion = bf16[512,2048]{1,0:T(8,128)(2,1)} fusion(bf16[2048,512]{0,1:T(8,128)(2,1)} %reduce-scatter.2.cloned.1.call-done, bf16[512,2048]{1,0:T(8,128)(2,1)S(1)} %copy-done.1, f32[2048]{0:T(1024)S(1)} %convert_element_type.35, f32[512]{0:T(512)S(1)} %add_rsqrt_fusion), kind=kLoop, calls=%fused_computation.12 | loop fusion | flops 6291456 | bytes 6301696 | tf_op jit(solution)/shard_map/convert_element_type | solution.py:114
  (5 shorter events, 0.0 us)
Async XLA Ops:
  6.5 2.3 copy-start.2
  6.5 251.4 %reduce-scatter.2.cloned.1.call-start = ((), (), s32[]{:S(2)}) async-start(), calls=%async_computation.1 | async-start | bytes 10485760 | tf_op jit(solution)/shard_map/reduce_scatter | solution.py:101
  56.9 2.0 copy-start
  101.0 48.2 %copy-start.3 = (bf16[512,256]{1,0:T(8,128)(2,1)S(1)}, bf16[512,256]{1,0:T(8,128)(2,1)}, u32[]{:S(2)}) copy-start(bf16[512,256]{1,0:T(8,128)(2,1)} %param.10) | copy-start | bytes 786436
  183.7 0.7 copy-start.4
  183.7 74.2 %copy-start.1 = (bf16[512,2048]{1,0:T(8,128)(2,1)S(1)}, bf16[512,2048]{1,0:T(8,128)(2,1)}, u32[]{:S(2)}) copy-start(bf16[512,2048]{1,0:T(8,128)(2,1)} %param.14) | copy-start | bytes 6291460
Sparse Core Ops, SparseCore 0:
  183.9 73.9 reduce-scatter.1
where the time goes:
time: 277 us
  matrix products  127 us (46%)
  waiting for transfers between devices  73.5 us (27%)
  other arithmetic  48.4 us (17%)
  between operations  13.5 us (5%)
  local copies, waits for them, and re-layouts  8.64 us (3%)
  blocking collectives  5.76 us (2%)
    reduce_scatter x1, waiting for transfers between devices, per_device(): lax.psum_scatter(lax.dot_general(out_weight, attended, (((0,), (1,)), (()...  73.5 us
    dot_general x1, matrix products, attend_block(): jnp.einsum('sghij,sgjd->sighd', weights.astype(jnp.bfloat16), old_values,...  48.1 us
    dot_general x1, matrix products, attend_block(): jnp.einsum('sighd,sgjd->sghij', grouped, old_keys, preferred_element_type...  47 us
    reduce_sum x1, other arithmetic, attend_block(): total = jnp.sum(weights, axis=-1)  40.9 us
    dot_general x1, matrix products, per_device(): lax.dot_general(out_weight, attended, (((0,), (1,)), ((), ())), preferred...  26.1 us
    psum x1, blocking collectives, per_device(): squares = lax.psum(jnp.sum(hidden * hidden, axis=1), 'tp')  5.76 us
  transfers between devices with their start and end apart: 1, of which 1 were waited for; matrix products, arithmetic and copies ran while one was open for 0% of the time, Pallas kernels for 0%

commit v1 on v0

--- a/solution.py
+++ b/solution.py
@@ -1,6 +1,10 @@
+import functools
+
 import jax
 import jax.numpy as jnp
 from jax import lax
+from jax.experimental import pallas as pl
+from jax.experimental.pallas import tpu as pltpu
 from jax.sharding import PartitionSpec as P
 
 D = 8192
@@ -114,6 +118,299 @@
     return scaled.astype(jnp.bfloat16)
 
 
+SEQS_PER_PART = 1
+HEADS_PER_BLOCK = 2
+KEY_CHUNK = 1024
+PIECES = 4
+MASKED = -1e30
+LOG2E = 1.4426950408889634
+MESH = pl.DeviceIdType.MESH
+
+
+def lane_max(tile, running):
+    for start in range(0, tile.shape[1], 128):
+        part = tile[:, start : start + 128]
+        running = part if running is None else jnp.maximum(running, part)
+    return running
+
+
+def attend_step(row, q_ref, k_ref, v_ref, nk_ref, nv_ref, att_ref, vx_ref, slots, column):
+    stored = k_ref.shape[1]
+    groups = q_ref.shape[1] // HD
+    rows = HEADS_PER_BLOCK * SPAN
+    blocks = groups // HEADS_PER_BLOCK
+    vx_ref[0:stored, 0:HD] = v_ref[0]
+    vx_ref[stored : stored + SPAN, 0:HD] = nv_ref[...]
+    factor = HD ** (-0.5) * LOG2E
+    chunks = [(start, KEY_CHUNK) for start in range(0, stored, KEY_CHUNK)] + [(stored, SPAN)]
+    position = lax.broadcasted_iota(jnp.int32, (SPAN, SPAN), 0)
+    causal_one = position >= lax.broadcasted_iota(jnp.int32, (SPAN, SPAN), 1)
+    causal = jnp.concatenate([causal_one] * HEADS_PER_BLOCK, axis=0)
+
+    def score_chunk(block, start, size, running):
+        first = block * HEADS_PER_BLOCK
+        heads = [q_ref[:, (first + i) * HD : (first + i + 1) * HD] for i in range(HEADS_PER_BLOCK)]
+        q = heads[0] if len(heads) == 1 else jnp.concatenate(heads, axis=0)
+        keys = nk_ref[...] if start == stored else k_ref[0, start : start + size, :]
+        tile = lax.dot_general(
+            q, keys, (((1,), (1,)), ((), ())), preferred_element_type=jnp.float32
+        )
+        if start == stored:
+            tile = jnp.where(causal, tile, MASKED)
+        slots[block % 2][:, start : start + size] = tile
+        return lane_max(tile, running)
+
+    running = None
+    for start, size in chunks:
+        running = score_chunk(0, start, size, running)
+    for block in range(blocks):
+        peak = jnp.max(running, axis=1, keepdims=True)
+        running = None
+        total = None
+        for start, size in chunks:
+            if block + 1 < blocks:
+                running = score_chunk(block + 1, start, size, running)
+            weights = jnp.exp2((slots[block % 2][:, start : start + size] - peak) * factor)
+            term = jnp.dot(
+                weights.astype(jnp.bfloat16),
+                vx_ref[start : start + size, :],
+                preferred_element_type=jnp.float32,
+            )
+            total = term if total is None else total + term
+        result = (total[:, :HD] / total[:, HD:]).astype(jnp.bfloat16)
+        for i in range(HEADS_PER_BLOCK):
+            where = column + (block * HEADS_PER_BLOCK + i) * HD
+            att_ref[pl.ds(row, SPAN), pl.ds(where, HD)] = result[i * SPAN : (i + 1) * SPAN]
+
+
+def fused_kernel(
+    q_ref, k_ref, v_ref, nk_ref, nv_ref, w_hbm, res_ref, gain_ref, out_hbm,
+    w_ref, att_ref, vx_ref, score_a, score_b,
+    s1_send, s1_recv, s2_send, s2_recv, hidden, staged, sq_send, sq_recv,
+    w_sem, s1_ss, s1_rs, s2_ss, s2_rs, sq_ss, sq_rs, out_sem,
+):
+    s, g = pl.program_id(0), pl.program_id(1)
+    local_kv = pl.num_programs(1)
+    parts = SEQS // SEQS_PER_PART
+    tokens = SEQS_PER_PART * SPAN
+    width = hidden.shape[2]
+    piece = width // PIECES
+    me = lax.axis_index("tp")
+    chip, core = me // 2, me % 2
+    sibling = chip * 2 + (1 - core)
+    across = (1 - chip) * 2 + core
+    diagonal = (1 - chip) * 2 + (1 - core)
+    w_pieces = w_sem.shape[0]
+    w_rows = w_ref.shape[0] // w_pieces
+
+    def w_copy(i):
+        span = pl.ds(i * w_rows, w_rows)
+        return pltpu.make_async_copy(w_hbm.at[span], w_ref.at[span], w_sem.at[i])
+
+    def remote(src, dst, ss, rs, device):
+        return pltpu.make_async_remote_copy(
+            src_ref=src, dst_ref=dst, send_sem=ss, recv_sem=rs,
+            device_id={"tp": device}, device_id_type=MESH,
+        )
+
+    def stage1(p, which, j):
+        col = pl.ds(which * width + j * piece, piece)
+        k = which * PIECES + j
+        return remote(
+            s1_send.at[:, col], s1_recv.at[p % 2, :, col], s1_ss.at[k], s1_rs.at[p % 2, k], sibling
+        )
+
+    def stage2(p, j):
+        col = pl.ds(j * piece, piece)
+        return remote(
+            s2_send.at[:, col], s2_recv.at[p % 2, :, col], s2_ss.at[j], s2_rs.at[p % 2, j], across
+        )
+
+    def squares(p):
+        return [
+            remote(sq_send.at[p], sq_recv.at[p, i], sq_ss.at[p, i], sq_rs.at[p, i], device)
+            for i, device in enumerate((sibling, across, diagonal))
+        ]
+
+    def out_copy(p):
+        return pltpu.make_async_copy(
+            staged.at[p % 2], out_hbm.at[pl.ds(p * tokens, tokens)], out_sem.at[p % 2]
+        )
+
+    @pl.when((s == 0) & (g == 0))
+    def _():
+        barrier = pltpu.get_barrier_semaphore()
+        for device in (sibling, across, diagonal):
+            pl.semaphore_signal(barrier, inc=1, device_id={"tp": device}, device_id_type=MESH)
+        for i in range(w_pieces):
+            w_copy(i).start()
+        vx_ref[:, HD:] = jnp.ones((vx_ref.shape[0], vx_ref.shape[1] - HD), jnp.bfloat16)
+        pl.semaphore_wait(barrier, 3)
+
+    attend_step(
+        pl.multiple_of(lax.rem(s, SEQS_PER_PART) * SPAN, SPAN),
+        q_ref, k_ref, v_ref, nk_ref, nv_ref, att_ref, vx_ref, (score_a, score_b),
+        pl.multiple_of(g * q_ref.shape[1], 128),
+    )
+
+    def project(owner, j):
+        col = pl.multiple_of(owner * width + j * piece, 128)
+        return jnp.dot(
+            att_ref[...], w_ref[:, pl.ds(col, piece)], preferred_element_type=jnp.float32
+        )
+
+    def project_part(p):
+        for j in range(PIECES):
+            s1_send[:, j * piece : (j + 1) * piece] = project(diagonal, j).astype(jnp.bfloat16)
+            stage1(p, 0, j).start()
+            own = project(across, j)
+            stage1(p, 0, j).wait_recv()
+            both = own + s1_recv[p % 2, :, j * piece : (j + 1) * piece].astype(jnp.float32)
+            s2_send[:, j * piece : (j + 1) * piece] = both.astype(jnp.bfloat16)
+            stage2(p, j).start()
+        for j in range(PIECES):
+            col = slice(width + j * piece, width + (j + 1) * piece)
+            s1_send[:, col] = project(sibling, j).astype(jnp.bfloat16)
+            stage1(p, 1, j).start()
+            own = slice(j * piece, (j + 1) * piece)
+            hidden[p % 2, :, own] = project(me, j) + res_ref[:, own].astype(jnp.float32)
+
+    def collect(p):
+        for j in range(PIECES):
+            stage1(p, 0, j).wait_send()
+            stage1(p, 1, j).wait()
+        lanes = None
+        for j in range(PIECES):
+            stage2(p, j).wait()
+            col = slice(j * piece, (j + 1) * piece)
+            other = slice(width + j * piece, width + (j + 1) * piece)
+            value = (
+                hidden[p % 2, :, col]
+                + s1_recv[p % 2, :, other].astype(jnp.float32)
+                + s2_recv[p % 2, :, col].astype(jnp.float32)
+            )
+            hidden[p % 2, :, col] = value
+            for start in range(0, piece, 128):
+                tile = value[:, start : start + 128]
+                lanes = tile * tile if lanes is None else lanes + tile * tile
+        for i in range(SEQS_PER_PART):
+            turned = jnp.transpose(lanes[i * SPAN : (i + 1) * SPAN])
+            row = jnp.sum(turned, axis=0, keepdims=True)
+            sq_send[p, :, i * SPAN : (i + 1) * SPAN] = jnp.broadcast_to(row, (8, SPAN))
+        for copy in squares(p):
+            copy.start()
+
+    def finish(p):
+        for copy in squares(p):
+            copy.wait()
+        summed = sq_send[p] + sq_recv[p, 0] + sq_recv[p, 1] + sq_recv[p, 2]
+        for i in range(SEQS_PER_PART):
+            row = summed[0:1, i * SPAN : (i + 1) * SPAN]
+            power = jnp.transpose(jnp.broadcast_to(row, (SPAN, SPAN))) / D
+            scale = lax.rsqrt(power + EPSILON)
+            for start in range(0, width, 128):
+                value = hidden[p % 2, i * SPAN : (i + 1) * SPAN, start : start + 128]
+                scaled = value * scale * gain_ref[:, start : start + 128].astype(jnp.float32)
+                staged[p % 2, i * SPAN : (i + 1) * SPAN, start : start + 128] = scaled.astype(
+                    jnp.bfloat16
+                )
+        out_copy(p).start()
+
+    p = s // SEQS_PER_PART
+
+    @pl.when((lax.rem(s, SEQS_PER_PART) == SEQS_PER_PART - 1) & (g == local_kv - 1))
+    def _():
+        @pl.when(p == 0)
+        def _():
+            for i in range(w_pieces):
+                w_copy(i).wait()
+
+        @pl.when(p > 0)
+        def _():
+            collect(p - 1)
+
+        project_part(p)
+
+        @pl.when(p > 2)
+        def _():
+            out_copy(p - 3).wait()
+
+        @pl.when(p > 0)
+        def _():
+            finish(p - 1)
+
+        @pl.when(p == parts - 1)
+        def _():
+            collect(p)
+            if parts > 2:
+                out_copy(p - 2).wait()
+            finish(p)
+            if parts > 1:
+                out_copy(p - 1).wait()
+            out_copy(p).wait()
+
+
+def fused(queries, new_keys, new_values, cache_keys, cache_values, out_weight, residual, norm_gain):
+    length = cache_keys.shape[1] // (new_keys.shape[1] // HD)
+    local_kv = new_keys.shape[1] // HD
+    group_width = queries.shape[1] // local_kv
+    width = residual.shape[1]
+    parts = SEQS // SEQS_PER_PART
+    tokens = SEQS_PER_PART * SPAN
+    keys_all = length + SPAN
+    rows = HEADS_PER_BLOCK * SPAN
+    bf16, f32 = jnp.bfloat16, jnp.float32
+    dma = pltpu.SemaphoreType.DMA
+    return pl.pallas_call(
+        fused_kernel,
+        grid=(SEQS, local_kv),
+        out_shape=jax.ShapeDtypeStruct(residual.shape, bf16),
+        in_specs=[
+            pl.BlockSpec((SPAN, group_width), lambda s, g: (s, g)),
+            pl.BlockSpec((1, length, HD), lambda s, g: (s, g, 0)),
+            pl.BlockSpec((1, length, HD), lambda s, g: (s, g, 0)),
+            pl.BlockSpec((SPAN, HD), lambda s, g: (s, g)),
+            pl.BlockSpec((SPAN, HD), lambda s, g: (s, g)),
+            pl.BlockSpec(memory_space=pl.ANY),
+            pl.BlockSpec((tokens, width), lambda s, g: (s // SEQS_PER_PART, 0)),
+            pl.BlockSpec((1, width), lambda s, g: (0, 0)),
+        ],
+        out_specs=pl.BlockSpec(memory_space=pl.ANY),
+        scratch_shapes=[
+            pltpu.VMEM(out_weight.shape, bf16),
+            pltpu.VMEM((tokens, queries.shape[1]), bf16),
+            pltpu.VMEM((keys_all, 2 * HD), bf16),
+            pltpu.VMEM((rows, keys_all), f32),
+            pltpu.VMEM((rows, keys_all), f32),
+            pltpu.VMEM((tokens, 2 * width), bf16),
+            pltpu.VMEM((2, tokens, 2 * width), bf16),
+            pltpu.VMEM((tokens, width), bf16),
+            pltpu.VMEM((2, tokens, width), bf16),
+            pltpu.VMEM((2, tokens, width), f32),
+            pltpu.VMEM((2, tokens, width), bf16),
+            pltpu.VMEM((parts, 8, tokens), f32),
+            pltpu.VMEM((parts, 3, 8, tokens), f32),
+            dma((8,)),
+            dma((2 * PIECES,)),
+            dma((2, 2 * PIECES)),
+            dma((PIECES,)),
+            dma((2, PIECES)),
+            dma((parts, 3)),
+            dma((parts, 3)),
+            dma((2,)),
+        ],
+        compiler_params=pltpu.CompilerParams(
+            collective_id=0,
+            has_side_effects=True,
+            vmem_limit_bytes=67043328,
+            dimension_semantics=("arbitrary", "arbitrary"),
+        ),
+    )(
+        queries, cache_keys, cache_values, new_keys, new_values, out_weight, residual,
+        norm_gain.reshape(1, -1),
+    )
+
+
 def solution(mesh):
     in_specs = (
         P("dp", "tp"),
@@ -127,5 +424,5 @@
     )
     out_specs = P("dp", "tp")
     return jax.shard_map(
-        per_device, mesh=mesh, in_specs=in_specs, out_specs=out_specs, check_vma=False
-    )
+        fused if mesh.shape["tp"] == 4 else per_device, mesh=mesh, in_specs=in_specs, out_specs=out_specs, check_vma=False
+    )

time: 277 us -> 108 us (0.39)
  matrix products: 127 us -> 0 us
  Pallas kernels: 0 us -> 103 us
  waiting for transfers between devices: 73.5 us -> 0 us
  other arithmetic: 48.4 us -> 0 us
  between operations: 13.5 us -> 0.01 us
  blocking collectives: 5.76 us -> 0 us
  local copies, waits for them, and re-layouts: 8.64 us -> 4.45 us
    dot_general x5 -> x0, matrix products: 127 us -> none  [the longest x1 48.1 us: attend_block(): jnp.einsum('sghij,sgjd->sighd', weights.astype(jnp.bfloat16), old_values,...]
    pallas_call x0 -> x1, Pallas kernels: none -> 103 us  [fused(): pl.pallas_call(fused_kernel, grid=(SEQS, local_kv), out_shape=jax.ShapeDt...]
    reduce_scatter x1 -> x0, waiting for transfers between devices: 73.5 us -> none  [per_device(): lax.psum_scatter(lax.dot_general(out_weight, attended, (((0,), (1,)), (()...]
    reduce_sum x3 -> x0, other arithmetic: 44.4 us -> none  [the longest x1 40.9 us: attend_block(): total = jnp.sum(weights, axis=-1)]
    psum x1 -> x0, blocking collectives: 5.76 us -> none  [per_device(): squares = lax.psum(jnp.sum(hidden * hidden, axis=1), 'tp')]
    convert_element_type x2 -> x0, other arithmetic: 3.97 us -> none  [the longest x1 3.96 us: per_device(): return scaled.astype(jnp.bfloat16)]
    convert_element_type x2 -> x0, local copies, waits for them, and re-layouts: 3.65 us -> none  [finish_rows(): return result.reshape(SEQS * SPAN, -1).astype(jnp.bfloat16)]
  transfers between devices with their start and end apart: 1 -> 0, of which waited for: 1 -> 0; matrix products, arithmetic and copies ran while one was open for 0% -> 0% of each run, Pallas kernels for 0% -> 0%
where the time goes in v1:
time: 108 us; the launch traced here: 107 us
  Pallas kernels  103 us (95%)
  local copies, waits for them, and re-layouts  4.45 us (4%)
    pallas_call x1, Pallas kernels, fused(): pl.pallas_call(fused_kernel, grid=(SEQS, local_kv), out_shape=jax.ShapeDt...  103 us
    unnamed x1, local copies, waits for them, and re-layouts  3.16 us

profile of v1, /device:TPU:0, one launch (start us, length us, event | category | flops | bytes accessed | tf_op | source)
XLA Modules:
  0.0 107.5 jit_solution(1877327550477731214)
XLA Ops:
  0.0 1.3 %reshape.3.gain_ref = bf16[1,2048]{1,0:T(2,128)(2,1)} reshape(bf16[2048]{0:T(1024)(128)(2,1)} %param.15) | data formatting | bytes 8192 | tf_op jit(solution)/shard_map/reshape | solution.py:410
  1.3 103.0 %shard_map.82 = bf16[512,2048]{1,0:T(8,128)(2,1)} custom-call(bf16[512,2048]{1,0:T(8,128)(2,1)} %q_ref.1, bf16[4,8192,128]{2,1,0:T(8,128)(2,1)} %k_ref.1, bf16[4,8192,128]{2,1,0:T(8,128)(2,1)} %v_ref.1, bf16[512,256]{1,0:T(8,128)(2,1)} %nk_ref.1, bf16[512,256]{1,0:T(8,128)(2,1)} %nv_ref.1, bf16[2048,8192]{1,0:T(8,128)(2,1)} %w_hbm.1, ...), custom_call_target="tpu_custom_call" | custom-call | tf_op jit(solution)/shard_map/pallas_call | solution.py:364
  104.3 3.2 %copy.10 = bf16[512,2048]{1,0:T(8,128)(2,1)} copy(bf16[512,2048]{1,0:T(8,128)(2,1)} %shard_map.82) | data formatting | bytes 4194304
